TPU v7x, 128 devices: a whole 4x4x4 slice. The times are simulated.
128 devices in a mesh: rep: 8 (over z, core), ep: 16 (over x, y).
Axes of the slice: x: 4, y: 4, z: 4, core: 2. Of those that a mesh axis runs over, the one named last changes fastest.
Arguments:
- latent_pages: bfloat16 [6144, 36864], P(('rep', 'ep')), may hold values from -4 to 4
- queries: bfloat16 [1024, 147456], P(('rep', 'ep')), may hold values from -4 to 4
- residual: bfloat16 [1024, 14336], P(('rep', 'ep')), may hold values from -6 to 6
- page_count: int32 [8, 16, 8], P(None, 'ep'), may hold values from 1 to 12, 48 in all within a row
- last_fill: int32 [8, 16, 8], P(None, 'ep'), may hold values from 4 to 64
- page_order: int32 [128, 48], P(('rep', 'ep')), may hold values from 0 to 47, each once within a row
- shed_slots: int32 [8, 16, 2], P(None, 'ep'), may hold values from 0 to 7, as said below
- shed_shift: int32 [16, 2], P('ep'), may hold values from 1 to 7
- expert_ids: int32 [4096, 8], P(('rep', 'ep')), may hold values from 0 to 127, all different within a row; in each aligned block of 32 rows (0 to 31, 32 to 63, ...) at most 4 rows name the same one
- gate_weight: float32 [4096, 8], P(('rep', 'ep')), may hold values from 0.05 to 0.5
- expert_home: int32 [128], replicated, may hold values from 0 to 127, each once
- norm_gain: float32 [3584], replicated, may hold values from 0.1 to 1.9
- value_up: bfloat16 [64, 512, 128], P('ep'), may hold values from -0.59765625 to 0.59765625
- out_weight: bfloat16 [8192, 3584], P('ep'), may hold values from -0.14941406 to 0.14941406
- expert_in: bfloat16 [128, 3584, 1024], P(('rep', 'ep')), may hold values from -0.09375 to 0.09375
- expert_out: bfloat16 [128, 1024, 3584], P(('rep', 'ep')), may hold values from -0.1875 to 0.1875
Outputs:
- attn_proj: bfloat16 [1024, 14336], P(('rep', 'ep'))
- layer_out: bfloat16 [1024, 14336], P(('rep', 'ep'))
Inputs may be any that keep to these rules, and one draw needn't show every extreme that they name: `shed_slots`: for each device, 2 different slots. `expert_ids`: each row names 8 different experts; in the rows of one device no expert is named by more than 4 rows.
All inputs are finite; a program needn't handle non-finite values.
Results may differ from a plain program's by a relative error of at most 0.015.
Values may be sent and summed in bfloat16 or wider, within the bound.
No kernel may reach another device: no remote copies, remote signals or barrier semaphores. Data moves between devices by JAX's collectives and lax.ppermute only.
A program may use at most 192 MiB of HBM per device.

v0:
```python
import jax
import jax.numpy as jnp
from jax import lax
from jax.sharding import Mesh
from jax.sharding import PartitionSpec as P

D = 3584
HEADS = 64
LAT = 512
KVW = 576
VHEAD = 128
TOP = 8
PAGE = 64
SPEC = 4
MAXP = 12
REQ_DEV = 8
PAGES_DEV = 48
EP = ("ep_0", "ep_1")
REP_EP = ("rep", "ep_0", "ep_1")
SCORE_SCALE = 192.0 ** (-0.5)
NORM_EPS = 0.25


def shifted(value, axis, steps):
    count = lax.axis_size(axis)
    pairs = [(source, (source + steps) % count) for source in range(count)]
    return lax.ppermute(value, axis, pairs)


def own_rows_2(terms, axes):
    so_far = terms.astype(jnp.bfloat16)
    for axis in axes:
        so_far = lax.psum_scatter(so_far, axis, scatter_dimension=0, tiled=True)
    return so_far.astype(jnp.float32)


def attend(key_block, query_block, lengths):
    request_count = key_block.shape[0]
    key_rows = key_block.reshape(request_count, MAXP * PAGE, KVW)
    query_rows = query_block.reshape(request_count, SPEC * HEADS, KVW)
    scores = (
        jnp.einsum("rqc,rkc->rqk", query_rows, key_rows, preferred_element_type=jnp.float32)
        * SCORE_SCALE
    )
    position = jnp.arange(MAXP * PAGE, dtype=jnp.int32)
    offset = jnp.arange(SPEC * HEADS, dtype=jnp.int32) // HEADS
    visible_end = lengths[:, None] - SPEC + 1 + offset[None, :]
    visible = position[None, None, :] < visible_end[:, :, None]
    scores = jnp.where(visible, scores, -1e30)
    exponent = jnp.exp(scores - jnp.max(scores, axis=2, keepdims=True))
    probability = (exponent / jnp.sum(exponent, axis=2, keepdims=True)).astype(jnp.bfloat16)
    latent = jnp.einsum(
        "rqk,rkl->rql", probability, key_rows[:, :, :LAT], preferred_element_type=jnp.float32
    )
    return latent.astype(jnp.bfloat16).reshape(request_count, SPEC * HEADS * LAT)


def fill_slots(arrived, picker, present, own_rows):
    return jnp.where(present[:, None], arrived[picker], own_rows)


def per_device(
    latent_pages,
    queries,
    residual,
    page_count,
    last_fill,
    page_order,
    shed_slots,
    shed_shift,
    expert_ids,
    gate_weight,
    expert_home,
    norm_gain,
    value_up,
    out_weight,
    expert_in,
    expert_out,
):
    rep_count = lax.axis_size("rep")
    col_count = lax.axis_size(EP)
    device_count = rep_count * col_count
    replica = lax.axis_index("rep")
    lengths = (page_count[:, 0, :] - 1) * PAGE + last_fill[:, 0, :]
    shed_table = shed_slots[:, 0, :]
    own_counts = page_count[replica, 0, :]
    offsets = jnp.cumsum(own_counts) - own_counts
    page_steps = jnp.arange(MAXP, dtype=jnp.int32)
    positions = jnp.minimum(offsets[:, None] + page_steps[None, :], PAGES_DEV - 1)
    own_keys = latent_pages[page_order[0][positions]].reshape(REQ_DEV, MAXP * PAGE * KVW)
    own_lengths = lengths[replica]
    own_sheds = shed_table[replica]
    shifts = shed_shift[0]
    matches = own_sheds[None, :] == jnp.arange(REQ_DEV, dtype=jnp.int32)[:, None]
    present = jnp.any(matches, axis=1)
    picker = jnp.argmax(matches, axis=1)
    own_latent = attend(own_keys, queries, own_lengths)
    tokens_dev = REQ_DEV * SPEC
    heads_dev = value_up.shape[0]
    token_latent = own_latent.reshape(tokens_dev, HEADS * LAT)
    regrouped = lax.all_to_all(token_latent, EP, split_axis=1, concat_axis=0, tiled=True)
    row_block = regrouped.reshape(tokens_dev * lax.axis_size(EP), heads_dev, LAT)
    lifted = jnp.einsum(
        "thl,hlv->thv", row_block, value_up, preferred_element_type=jnp.float32
    ).astype(jnp.bfloat16)
    branch = own_rows_2(
        jnp.dot(
            lifted.reshape(tokens_dev * lax.axis_size(EP), heads_dev * VHEAD),
            out_weight,
            preferred_element_type=jnp.float32,
        ),
        EP,
    )
    own_branch = branch.astype(jnp.bfloat16).reshape(REQ_DEV, SPEC * D)
    arrived = jnp.concatenate((own_branch[own_sheds], residual[own_sheds]), axis=1)
    for bit_level in range(rep_count.bit_length() - 1):
        moved = shifted(arrived, "rep", 1 << bit_level)
        taking = shifts // (1 << bit_level) % 2 == 1
        arrived = jnp.where(taking[:, None], moved, arrived)
    served_branch = fill_slots(arrived[:, : SPEC * D], picker, present, own_branch)
    served_rest = fill_slots(arrived[:, SPEC * D :], picker, present, residual)
    branch = served_branch.reshape(tokens_dev, D).astype(jnp.float32)
    mixed = served_rest.reshape(tokens_dev, D).astype(jnp.float32) + branch
    square = jnp.mean(mixed * mixed, axis=1, keepdims=True)
    normed = (mixed * lax.rsqrt(square + NORM_EPS) * norm_gain).astype(jnp.bfloat16)
    capacity = max(4, 2 * tokens_dev * TOP // device_count)
    flat_ids = expert_ids.reshape(-1)
    target = expert_home[flat_ids]
    hits = (target[:, None] == jnp.arange(device_count, dtype=jnp.int32)[None, :]).astype(jnp.int32)
    before = jnp.sum((jnp.cumsum(hits, axis=0) - hits) * hits, axis=1)
    slot_index = target * capacity + before
    buffer_rows = jnp.arange(device_count * capacity, dtype=jnp.int32)
    landing = buffer_rows[:, None, None] == slot_index.reshape(tokens_dev, TOP)[None, :, :]
    chooser = jnp.any(landing, axis=2).astype(jnp.bfloat16)
    outgoing_tokens = jnp.dot(chooser, normed, preferred_element_type=jnp.float32).astype(
        jnp.bfloat16
    )
    incoming = lax.all_to_all(
        outgoing_tokens.reshape(device_count, capacity, D),
        REP_EP,
        split_axis=0,
        concat_axis=0,
        tiled=True,
    )
    inner_act = jax.nn.silu(
        jnp.dot(
            incoming.reshape(device_count * capacity, D),
            expert_in[0],
            preferred_element_type=jnp.float32,
        )
    ).astype(jnp.bfloat16)
    outer_out = jnp.dot(inner_act, expert_out[0], preferred_element_type=jnp.float32).astype(
        jnp.bfloat16
    )
    returned = lax.all_to_all(
        outer_out.reshape(device_count, capacity, D),
        REP_EP,
        split_axis=0,
        concat_axis=0,
        tiled=True,
    )
    picked = (
        returned.reshape(device_count * capacity, D)[slot_index]
        .reshape(tokens_dev, TOP, D)
        .astype(jnp.float32)
    )
    moe_sum = jnp.sum(gate_weight[:, :, None] * picked, axis=1)
    attn_proj = served_branch
    layer_out = (mixed + moe_sum).astype(jnp.bfloat16).reshape(REQ_DEV, SPEC * D)
    return (attn_proj, layer_out)


def solution(mesh):
    torus = Mesh(mesh.devices.reshape(mesh.shape["rep"], 4, 4), ("rep", "ep_0", "ep_1"))
    return jax.shard_map(
        per_device,
        mesh=torus,
        in_specs=(
            P(REP_EP, None),
            P(REP_EP, None),
            P(REP_EP, None),
            P(None, EP, None),
            P(None, EP, None),
            P(REP_EP, None),
            P(None, EP, None),
            P(EP, None),
            P(REP_EP, None),
            P(REP_EP, None),
            P(),
            P(),
            P(EP, None, None),
            P(EP, None),
            P(REP_EP, None, None),
            P(REP_EP, None, None),
        ),
        out_specs=(P(REP_EP, None), P(REP_EP, None)),
        check_vma=False,
    )
```

profile of v0, /device:TPU:1, one launch (start us, length us, event | category | flops | bytes accessed | tf_op | source)
XLA Modules:
  0.0 374.2 jit_solution(15845066801113839272)
XLA Ops:
  7.2 0.6 and_select_fusion
  7.8 1.6 fusion.45
  9.3 0.2 reduce-window.18
  9.5 0.7 bitcast_subtract_fusion.1
  10.4 1.6 gather_fusion
  12.0 0.7 reshape.439
  12.7 0.8 copy.40
  13.5 0.7 reshape.420
  14.1 0.7 compare_select_fusion.3
  14.8 0.7 pad_clamp_fusion.1
  15.5 8.1 %gather_fusion.1 = bf16[96,36864]{1,0:T(8,128)(2,1)} fusion(bf16[48,36864]{1,0:T(8,128)(2,1)S(1)} %copy-done, s32[1024]{0:T(1024)S(1)} %get-tuple-element.18), kind=kCustom, calls=%fused_computation.1 | custom fusion | bytes 14156160 | tf_op jit(solution)/shard_map/gather | solution.py:90
  23.6 14.2 %reshape_reshape.4 = bf16[8,768,576]{2,1,0:T(8,128)(2,1)} reshape(bf16[96,36864]{1,0:T(8,128)(2,1)} %gather_fusion.1) | data formatting | bytes 14155776 | tf_op jit(solution)/shard_map/reshape;reshape | solution.py:39
  37.8 2.7 reshape.501
  40.5 3.3 reshape.416
  43.9 10.7 %fusion.51 = (f32[8,256]{1,0:T(8,128)S(1)}, f32[8,256,768]{1,2,0:T(8,128)}) fusion(s32[8,256]{1,0:T(8,128)S(1)} %broadcast_add_fusion.1, bf16[8,768,576]{2,1,0:T(8,128)(2,1)} %reshape_reshape.4, bf16[8,256,576]{2,1,0:T(8,128)(2,1)} %reshape.416), kind=kOutput, calls=%fused_computation.115 | convolution fusion | flops 1819804416 | bytes 15745024 | tf_op jit(solution)/shard_map/sub | solution.py:50
  54.6 7.8 %fusion.18 = bf16[8,256,512]{2,1,0:T(8,128)(2,1)} fusion(bf16[8,768,576]{2,1,0:T(8,128)(2,1)} %reshape_reshape.4, f32[8,256,768]{1,2,0:T(8,128)} %get-tuple-element.16, f32[8,256]{1,0:T(8,128)S(1)} %get-tuple-element.15), kind=kOutput, calls=%fused_computation.32 | convolution fusion | flops 1614807040 | bytes 14688256 | tf_op jit(solution)/shard_map/rqk,rkl->rql/dot_general | solution.py:52
  62.4 3.1 all_to_all.18
  65.5 1.2 copy.36
  66.7 34.7 %all_to_all.26 = bf16[32,16,2048]{2,0,1:T(8,128)(2,1)S(1)} all-to-all(bf16[32,16,2048]{2,0,1:T(8,128)(2,1)S(1)} %copy.36), channel_id=1, replica_groups=mesh['rep'=8,'ep_0'=4,'ep_1'=4] {'ep_0','ep_1'}, dimensions={1} | all-to-all | bytes 4194304 | tf_op jit(solution)/shard_map/all_to_all | solution.py:101
  101.3 2.8 reshape.417
  104.1 2.6 fusion.23
  106.8 3.9 %convolution_convert_fusion.1 = bf16[512,3584]{1,0:T(8,128)(2,1)} fusion(bf16[512,512]{0,1:T(8,128)(2,1)S(1)} %bitcast.103, bf16[512,3584]{1,0:T(8,128)(2,1)S(1)} %copy-done.4), kind=kOutput, calls=%fused_computation.21 | convolution fusion | flops 1880883200 | bytes 7864320 | tf_op jit(solution)/shard_map/dot_general | solution.py:107
  110.7 43.1 %reduce-scatter.3.cloned.1.call-done = bf16[128,3584]{1,0:T(8,128)(2,1)} async-done(((bf16[512,3584]{1,0:T(8,128)(2,1)}), bf16[128,3584]{1,0:T(8,128)(2,1)}) %reduce-scatter.3.cloned.1.call-update) | async-done | bytes 917520 | tf_op jit(solution)/shard_map/reduce_scatter | solution.py:33
  153.9 0.2 dynamic-slice_reduce_fusion
  154.1 1.9 gather_fusion.6
  156.0 0.1 copy.41
  156.1 0.2 fusion.31
  156.4 0.2 fusion.33
  156.7 0.6 gather_fusion.3
  157.3 0.6 iota_reduce_fusion
  158.0 20.0 %reduce-scatter.5.cloned.1.call-done = bf16[32,3584]{1,0:T(8,128)(2,1)} async-done(((bf16[128,3584]{1,0:T(8,128)(2,1)}), bf16[32,3584]{1,0:T(8,128)(2,1)}) %reduce-scatter.5.cloned.1.call-update) | async-done | bytes 229392 | tf_op jit(solution)/shard_map/reduce_scatter | solution.py:33
  178.0 1.1 reshape.419
  179.1 0.6 gather_fusion.2
  179.9 3.2 collective-permute-start
  183.0 1.8 collective-permute-done
  184.8 0.2 broadcast_select_fusion
  185.0 1.4 collective-permute-start.1
  186.4 0.2 fusion.28
  186.6 3.3 collective-permute-done.1
  189.9 0.2 broadcast_select_fusion.1
  190.2 1.4 collective-permute-start.2
  191.8 0.1 broadcast_in_dim.75
  191.9 3.5 collective-permute-done.2
  195.4 0.2 broadcast_select_fusion.2
  195.7 0.7 gather_fusion.4
  196.4 0.7 gather_fusion.5
  197.1 0.2 gather.35
  197.3 0.8 select_convert_fusion
  198.1 0.1 reshape.427
  198.3 0.3 multiply_reduce_fusion
  198.6 3.0 convolution_convert_fusion
  201.6 7.0 %reshape.422 = bf16[128,4,3584]{2,1,0:T(4,128)(2,1)} reshape(bf16[512,3584]{1,0:T(8,128)(2,1)} %convolution_convert_fusion) | data formatting | bytes 7340032 | tf_op jit(solution)/shard_map/reshape | solution.py:139
  208.6 56.8 %all_to_all.27 = bf16[128,4,3584]{2,1,0:T(4,128)(2,1)} all-to-all(bf16[128,4,3584]{2,1,0:T(4,128)(2,1)} %reshape.422), channel_id=1, replica_groups=mesh['rep'=8,'ep_0'=4,'ep_1'=4] {'rep','ep_0','ep_1'}, dimensions={0} | all-to-all | bytes 7340032 | tf_op jit(solution)/shard_map/all_to_all | solution.py:138
  265.3 6.7 %reshape.423 = bf16[512,3584]{1,0:T(8,128)(2,1)} reshape(bf16[128,4,3584]{2,1,0:T(4,128)(2,1)} %all_to_all.27) | data formatting | bytes 7340032 | tf_op jit(solution)/shard_map/reshape | solution.py:147
  272.1 16.0 %fusion.7 = bf16[512,3584]{1,0:T(8,128)(2,1)} fusion(bf16[1,1024,3584]{2,1,0:T(8,128)(2,1)} %param.31, bf16[512,3584]{1,0:T(8,128)(2,1)} %reshape.423, bf16[1,3584,1024]{2,1,0:T(8,128)(2,1)} %param.30), kind=kOutput, calls=%fused_computation.19 | convolution fusion | flops 7520649216 | bytes 22020096 | tf_op jit(solution)/shard_map/dot_general | solution.py:152
  288.0 7.0 %reshape.424 = bf16[128,4,3584]{2,1,0:T(4,128)(2,1)} reshape(bf16[512,3584]{1,0:T(8,128)(2,1)} %fusion.7) | data formatting | bytes 7340032 | tf_op jit(solution)/shard_map/reshape | solution.py:156
  295.0 5.1 %all-to-all-start.2 = ((bf16[128,4,3584]{2,1,0:T(4,128)(2,1)}), bf16[128,4,3584]{2,1,0:T(4,128)(2,1)}, u32[]{:S(2)}, u32[]{:S(2)}) async-start(bf16[128,4,3584]{2,1,0:T(4,128)(2,1)} %reshape.424), calls=%async_computation.4 | async-start | bytes 7340032 | tf_op jit(solution)/shard_map/all_to_all | solution.py:155
  300.3 0.6 pad_clamp_fusion
  300.9 45.6 %all-to-all-done.2 = bf16[128,4,3584]{2,1,0:T(4,128)(2,1)} async-done(((bf16[128,4,3584]{2,1,0:T(4,128)(2,1)}), bf16[128,4,3584]{2,1,0:T(4,128)(2,1)}, u32[]{:S(2)}, u32[]{:S(2)}) %all-to-all-start.2) | async-done | bytes 3670048 | tf_op jit(solution)/shard_map/all_to_all | solution.py:155
  346.5 6.7 %reshape.425 = bf16[512,3584]{1,0:T(8,128)(2,1)} reshape(bf16[128,4,3584]{2,1,0:T(4,128)(2,1)} %all-to-all-done.2) | data formatting | bytes 7340032 | tf_op jit(solution)/shard_map/reshape | solution.py:163
  353.2 7.6 %gather_fusion.7 = bf16[256,3584]{1,0:T(8,128)(2,1)} fusion(bf16[512,3584]{1,0:T(8,128)(2,1)} %reshape.425, s32[1024]{0:T(1024)} %pad_clamp_fusion), kind=kCustom, calls=%fused_computation.7 | custom fusion | bytes 3671040 | tf_op jit(solution)/shard_map/gather | solution.py:163
  360.8 3.0 fusion.11
  363.7 1.8 add_convert_fusion
  365.5 1.8 reshape.426
  (59 shorter events, 1.2 us)
Async XLA Ops:
  7.2 8.3 %copy-start = (bf16[48,36864]{1,0:T(8,128)(2,1)S(1)}, bf16[48,36864]{1,0:T(8,128)(2,1)}, u32[]{:S(2)}) copy-start(bf16[48,36864]{1,0:T(8,128)(2,1)} %param.16) | copy-start | bytes 10616836
  7.2 146.7 %reduce-scatter.3.cloned.1.call-start = ((), (), s32[]{:S(2)}) async-start(), calls=%async_computation.5 | async-start | bytes 4587520 | tf_op jit(solution)/shard_map/reduce_scatter | solution.py:33
  40.5 3.4 copy-start.9
  40.5 3.4 copy-start.10
  66.7 37.5 %copy-start.13 = (bf16[4,512,128]{2,1,0:T(8,128)(2,1)S(1)}, bf16[4,512,128]{2,1,0:T(8,128)(2,1)}, u32[]{:S(2)}) copy-start(bf16[4,512,128]{2,1,0:T(8,128)(2,1)} %param.28) | copy-start | bytes 1572868
  104.1 2.7 copy-start.4
  110.7 43.3 %copy-start.11 = (s32[8,1,2]{0,2,1:T(2,128)S(1)}, s32[8,1,2]{0,2,1:T(2,128)}, u32[]{:S(2)}) copy-start(s32[8,1,2]{0,2,1:T(2,128)} %param.22) | copy-start | bytes 196
  110.7 43.4 %copy-start.2 = (s32[128]{0:T(128)S(1)}, s32[128]{0:T(128)}, u32[]{:S(2)}) copy-start(s32[128]{0:T(128)} %param.26) | copy-start | bytes 1540
  110.7 46.0 %copy-start.5 = (bf16[8,14336]{1,0:T(8,128)(2,1)S(1)}, bf16[8,14336]{1,0:T(8,128)(2,1)}, u32[]{:S(2)}) copy-start(bf16[8,14336]{1,0:T(8,128)(2,1)} %param.18) | copy-start | bytes 688132
  110.7 47.3 %copy-start.12 = (s32[1,2]{1,0:T(1,128)S(1)}, s32[1,2]{1,0:T(1,128)}, u32[]{:S(2)}) copy-start(s32[1,2]{1,0:T(1,128)} %param.23) | copy-start | bytes 28
  110.7 67.3 %reduce-scatter.5.cloned.1.call-start = ((), (), s32[]{:S(2)}) async-start(), calls=%async_computation.6 | async-start | bytes 1146880 | tf_op jit(solution)/shard_map/reduce_scatter | solution.py:33
  179.9 5.0 %collective-permute-start = (bf16[2,28672]{1,0:T(2,128)(2,1)S(1)}, bf16[2,28672]{1,0:T(2,128)(2,1)S(1)}, u32[]{:S(2)}, u32[]{:S(2)}) collective-permute-start(bf16[2,28672]{1,0:T(2,128)(2,1)S(1)} %constant_dynamic-update-slice_fusion), channel_id=1, source_target_pairs={{0,16},{16,32},{32,48},{48,64},{64,80},{80,96},{96,112},{112,0},{1... | collective-permute-start | bytes 344072 | tf_op jit(solution)/shard_map/ppermute | solution.py:27
  185.0 4.9 %collective-permute-start.1 = (bf16[2,28672]{1,0:T(2,128)(2,1)S(1)}, bf16[2,28672]{1,0:T(2,128)(2,1)S(1)}, u32[]{:S(2)}, u32[]{:S(2)}) collective-permute-start(bf16[2,28672]{1,0:T(2,128)(2,1)S(1)} %broadcast_select_fusion), channel_id=1, source_target_pairs={{0,32},{16,48},{32,64},{48,80},{64,96},{80,112},{96,0},{112,16},{1... | collective-permute-start | bytes 344072 | tf_op jit(solution)/shard_map/ppermute | solution.py:27
  190.2 5.2 %collective-permute-start.2 = (bf16[2,28672]{1,0:T(2,128)(2,1)S(1)}, bf16[2,28672]{1,0:T(2,128)(2,1)S(1)}, u32[]{:S(2)}, u32[]{:S(2)}) collective-permute-start(bf16[2,28672]{1,0:T(2,128)(2,1)S(1)} %broadcast_select_fusion.1), channel_id=1, source_target_pairs={{0,64},{16,80},{32,96},{48,112},{64,0},{80,16},{96,32},{112,48},{1... | collective-permute-start | bytes 344072 | tf_op jit(solution)/shard_map/ppermute | solution.py:27
  195.6 2.6 copy-start.6
  196.4 2.2 copy-start.7
  198.5 10.0 %copy-start.3 = (f32[32,3584]{1,0:T(8,128)}, f32[32,3584]{1,0:T(8,128)S(1)}, u32[]{:S(2)}) copy-start(f32[32,3584]{1,0:T(8,128)S(1)} %get-tuple-element.5) | copy-start | bytes 1376260
  295.0 5.1 %copy-start.8 = (f32[32,8]{0,1:T(8,128)S(1)}, f32[32,8]{0,1:T(8,128)}, u32[]{:S(2)}) copy-start(f32[32,8]{0,1:T(8,128)} %param.25) | copy-start | bytes 3076
  295.0 51.4 %all-to-all-start.2 = ((bf16[128,4,3584]{2,1,0:T(4,128)(2,1)}), bf16[128,4,3584]{2,1,0:T(4,128)(2,1)}, u32[]{:S(2)}, u32[]{:S(2)}) async-start(bf16[128,4,3584]{2,1,0:T(4,128)(2,1)} %reshape.424), calls=%async_computation.4 | async-start | bytes 7340032 | tf_op jit(solution)/shard_map/all_to_all | solution.py:155
  353.2 14.2 %copy-start.1 = (bf16[48,36864]{1,0:T(8,128)(2,1)S(1)}, bf16[48,36864]{1,0:T(8,128)(2,1)}, u32[]{:S(2)}) copy-start(bf16[48,36864]{1,0:T(8,128)(2,1)} %param.16) | copy-start | bytes 10616836
Sparse Core Ops, SparseCore 0:
  110.8 43.0 reduce-scatter.2
  156.3 21.6 reduce-scatter.4
where the time goes:
time: 376 us; the launch traced here: 374 us
  waiting for transfers between devices  117 us (31%)
  blocking collectives  91.4 us (24%)
  local copies, waits for them, and re-layouts  83 us (22%)
  matrix products  43.9 us (12%)
  between operations  14.3 us (4%)
  other arithmetic  13 us (3%)
  starting transfers between devices  11.2 us (3%)
    reduce_scatter x2, waiting for transfers between devices, own_rows_2(): so_far = lax.psum_scatter(so_far, axis, scatter_dimension=0, tiled=True)  63.1 us
    all_to_all x1, blocking collectives, per_device(): lax.all_to_all(outgoing_tokens.reshape(device_count, capacity, D), REP_EP...  56.8 us
    all_to_all x1, waiting for transfers between devices, per_device(): lax.all_to_all(outer_out.reshape(device_count, capacity, D), REP_EP, spli...  45.6 us
    all_to_all x1, blocking collectives, per_device(): lax.all_to_all(token_latent, EP, split_axis=1, concat_axis=0, tiled=True)  34.7 us
    dot_general x1, matrix products, per_device(): jnp.dot(inner_act, expert_out[0], preferred_element_type=jnp.float32)  16 us
    another operation x1, local copies, waits for them, and re-layouts, attend(): key_rows = key_block.reshape(request_count, MAXP * PAGE, KVW)  14.2 us
    sub x1, matrix products, attend(): exponent = jnp.exp(scores - jnp.max(scores, axis=2, keepdims=True))  10.7 us
    ppermute x3, waiting for transfers between devices, shifted(): return lax.ppermute(value, axis, pairs)  8.65 us
  transfers between devices with their start and end apart: 6, of which 6 were waited for; matrix products, arithmetic and copies ran while one was open for 1% of the time, Pallas kernels for 0%

commit v1 on v0

--- a/solution.py
+++ b/solution.py
@@ -98,7 +98,9 @@
     tokens_dev = REQ_DEV * SPEC
     heads_dev = value_up.shape[0]
     token_latent = own_latent.reshape(tokens_dev, HEADS * LAT)
-    regrouped = lax.all_to_all(token_latent, EP, split_axis=1, concat_axis=0, tiled=True)
+    parts = jnp.split(token_latent, lax.axis_size(EP), axis=1)
+    received = lax.all_to_all(jnp.stack(parts), EP, 0, 0)
+    regrouped = jnp.concatenate(received, axis=0)
     row_block = regrouped.reshape(tokens_dev * lax.axis_size(EP), heads_dev, LAT)
     lifted = jnp.einsum(
         "thl,hlv->thv", row_block, value_up, preferred_element_type=jnp.float32

time: 376 us -> 373 us (level)
    another operation x3 -> x6, local copies, waits for them, and re-layouts: 0.02 us -> 5.68 us  [the longest x1 2.87 us: per_device(): token_latent = own_latent.reshape(tokens_dev, HEADS * LAT)]
    all_to_all x2 -> x0, local copies, waits for them, and re-layouts: 4.25 us -> none  [per_device(): lax.all_to_all(token_latent, EP, split_axis=1, concat_axis=0, tiled=True)]
where the time goes in v1:
time: 373 us; the launch traced here: 372 us
  waiting for transfers between devices  117 us (31%)
  blocking collectives  91.3 us (24%)
  local copies, waits for them, and re-layouts  81.4 us (22%)
  matrix products  43.9 us (12%)
  between operations  14.5 us (4%)
  other arithmetic  11.7 us (3%)
  starting transfers between devices  11.3 us (3%)
    reduce_scatter x2, waiting for transfers between devices, own_rows_2(): so_far = lax.psum_scatter(so_far, axis, scatter_dimension=0, tiled=True)  63.1 us
    all_to_all x1, blocking collectives, per_device(): lax.all_to_all(outgoing_tokens.reshape(device_count, capacity, D), REP_EP...  56.8 us
    all_to_all x1, waiting for transfers between devices, per_device(): lax.all_to_all(outer_out.reshape(device_count, capacity, D), REP_EP, spli...  45.6 us
    all_to_all x1, blocking collectives, per_device(): received = lax.all_to_all(jnp.stack(parts), EP, 0, 0)  34.5 us
    dot_general x1, matrix products, per_device(): jnp.dot(inner_act, expert_out[0], preferred_element_type=jnp.float32)  16 us
    another operation x1, local copies, waits for them, and re-layouts, attend(): key_rows = key_block.reshape(request_count, MAXP * PAGE, KVW)  14.2 us
    sub x1, matrix products, attend(): exponent = jnp.exp(scores - jnp.max(scores, axis=2, keepdims=True))  10.7 us
    ppermute x3, waiting for transfers between devices, shifted(): return lax.ppermute(value, axis, pairs)  8.66 us
  transfers between devices with their start and end apart: 6, of which 6 were waited for; matrix products, arithmetic and copies ran while one was open for 1% of the time, Pallas kernels for 0%

profile of v1, /device:TPU:1, one launch (start us, length us, event | category | flops | bytes accessed | tf_op | source)
XLA Modules:
  0.0 371.6 jit_solution(14457541736659279521)
XLA Ops:
  7.2 0.6 and_select_fusion
  7.8 1.3 fusion.61
  9.1 0.2 reduce-window.18
  9.3 0.7 bitcast_subtract_fusion.1
  10.1 1.2 gather_fusion
  11.5 0.7 reshape.430
  12.1 0.8 copy.38
  12.9 0.7 reshape.411
  13.6 0.7 compare_select_fusion.3
  14.2 0.7 pad_clamp_fusion.1
  14.9 8.1 %gather_fusion.1 = bf16[96,36864]{1,0:T(8,128)(2,1)} fusion(bf16[48,36864]{1,0:T(8,128)(2,1)S(1)} %copy-done, s32[1024]{0:T(1024)S(1)} %get-tuple-element.18), kind=kCustom, calls=%fused_computation.1 | custom fusion | bytes 14156160 | tf_op jit(solution)/shard_map/gather | solution.py:90
  23.0 14.2 %reshape_reshape.9 = bf16[8,768,576]{2,1,0:T(8,128)(2,1)} reshape(bf16[96,36864]{1,0:T(8,128)(2,1)} %gather_fusion.1) | data formatting | bytes 14155776 | tf_op jit(solution)/shard_map/reshape;reshape | solution.py:39
  37.2 2.7 reshape.492
  40.0 3.3 reshape.408
  43.4 10.7 %fusion.67 = (f32[8,256]{1,0:T(8,128)S(1)}, f32[8,256,768]{1,2,0:T(8,128)}) fusion(s32[8,256]{1,0:T(8,128)S(1)} %broadcast_add_fusion.1, bf16[8,768,576]{2,1,0:T(8,128)(2,1)} %reshape_reshape.9, bf16[8,256,576]{2,1,0:T(8,128)(2,1)} %reshape.408), kind=kOutput, calls=%fused_computation.147 | convolution fusion | flops 1819804416 | bytes 15745024 | tf_op jit(solution)/shard_map/sub | solution.py:50
  54.0 7.8 %fusion.18 = bf16[8,256,512]{2,1,0:T(8,128)(2,1)} fusion(bf16[8,768,576]{2,1,0:T(8,128)(2,1)} %reshape_reshape.9, f32[8,256,768]{1,2,0:T(8,128)} %get-tuple-element.16, f32[8,256]{1,0:T(8,128)S(1)} %get-tuple-element.15), kind=kOutput, calls=%fused_computation.32 | convolution fusion | flops 1614807040 | bytes 14688256 | tf_op jit(solution)/shard_map/rqk,rkl->rql/dot_general | solution.py:52
  61.8 2.9 reshape_reshape.10
  65.0 34.5 %all_to_all.15 = bf16[16,32,2048]{2,1,0:T(8,128)(2,1)S(1)} all-to-all(bf16[16,32,2048]{2,1,0:T(8,128)(2,1)S(1)} %fusion.32), channel_id=1, replica_groups=mesh['rep'=8,'ep_0'=4,'ep_1'=4] {'ep_0','ep_1'}, dimensions={0} | all-to-all | bytes 4194304 | tf_op jit(solution)/shard_map/all_to_all | solution.py:102
  99.6 2.8 reshape_reshape.11
  102.3 2.6 fusion.23
  105.0 3.9 %convolution_convert_fusion.1 = bf16[512,3584]{1,0:T(8,128)(2,1)} fusion(bf16[512,512]{0,1:T(8,128)(2,1)S(1)} %bitcast.165, bf16[512,3584]{1,0:T(8,128)(2,1)S(1)} %copy-done.6), kind=kOutput, calls=%fused_computation.21 | convolution fusion | flops 1880883200 | bytes 7864320 | tf_op jit(solution)/shard_map/dot_general | solution.py:109
  109.0 43.1 %reduce-scatter.3.cloned.1.call-done = bf16[128,3584]{1,0:T(8,128)(2,1)} async-done(((bf16[512,3584]{1,0:T(8,128)(2,1)}), bf16[128,3584]{1,0:T(8,128)(2,1)}) %reduce-scatter.3.cloned.1.call-update) | async-done | bytes 917520 | tf_op jit(solution)/shard_map/reduce_scatter | solution.py:33
  152.1 0.2 dynamic-slice_reduce_fusion
  152.3 1.9 gather_fusion.6
  154.2 0.1 copy.39
  154.3 0.2 fusion.31
  154.6 0.2 fusion.49
  154.9 0.6 gather_fusion.3
  155.6 0.6 iota_reduce_fusion
  156.2 20.0 %reduce-scatter.5.cloned.1.call-done = bf16[32,3584]{1,0:T(8,128)(2,1)} async-done(((bf16[128,3584]{1,0:T(8,128)(2,1)}), bf16[32,3584]{1,0:T(8,128)(2,1)}) %reduce-scatter.5.cloned.1.call-update) | async-done | bytes 229392 | tf_op jit(solution)/shard_map/reduce_scatter | solution.py:33
  176.2 1.1 reshape.410
  177.4 0.6 gather_fusion.2
  178.1 3.1 collective-permute-start
  181.2 1.8 collective-permute-done
  183.0 0.2 broadcast_select_fusion
  183.2 1.3 collective-permute-start.1
  184.6 0.2 fusion.28
  184.8 3.3 collective-permute-done.1
  188.2 0.2 broadcast_select_fusion.1
  188.4 1.7 collective-permute-start.2
  190.0 0.1 fusion.52
  190.2 0.1 broadcast_in_dim.75
  190.3 3.5 collective-permute-done.2
  193.8 0.2 broadcast_select_fusion.2
  194.1 0.7 gather_fusion.4
  194.8 0.7 gather_fusion.5
  195.5 0.2 gather.35
  195.7 0.8 select_convert_fusion
  196.6 0.1 reshape.418
  196.7 0.3 multiply_reduce_fusion
  197.0 3.0 convolution_convert_fusion
  200.0 7.0 %reshape.413 = bf16[128,4,3584]{2,1,0:T(4,128)(2,1)} reshape(bf16[512,3584]{1,0:T(8,128)(2,1)} %convolution_convert_fusion) | data formatting | bytes 7340032 | tf_op jit(solution)/shard_map/reshape | solution.py:141
  207.0 56.8 %all_to_all.16 = bf16[128,4,3584]{2,1,0:T(4,128)(2,1)} all-to-all(bf16[128,4,3584]{2,1,0:T(4,128)(2,1)} %reshape.413), channel_id=1, replica_groups=mesh['rep'=8,'ep_0'=4,'ep_1'=4] {'rep','ep_0','ep_1'}, dimensions={0} | all-to-all | bytes 7340032 | tf_op jit(solution)/shard_map/all_to_all | solution.py:140
  263.8 6.7 %reshape.414 = bf16[512,3584]{1,0:T(8,128)(2,1)} reshape(bf16[128,4,3584]{2,1,0:T(4,128)(2,1)} %all_to_all.16) | data formatting | bytes 7340032 | tf_op jit(solution)/shard_map/reshape | solution.py:149
  270.5 16.0 %fusion.7 = bf16[512,3584]{1,0:T(8,128)(2,1)} fusion(bf16[1,1024,3584]{2,1,0:T(8,128)(2,1)} %param.31, bf16[512,3584]{1,0:T(8,128)(2,1)} %reshape.414, bf16[1,3584,1024]{2,1,0:T(8,128)(2,1)} %param.30), kind=kOutput, calls=%fused_computation.19 | convolution fusion | flops 7520649216 | bytes 22020096 | tf_op jit(solution)/shard_map/dot_general | solution.py:154
  286.5 7.0 %reshape.415 = bf16[128,4,3584]{2,1,0:T(4,128)(2,1)} reshape(bf16[512,3584]{1,0:T(8,128)(2,1)} %fusion.7) | data formatting | bytes 7340032 | tf_op jit(solution)/shard_map/reshape | solution.py:158
  293.5 5.1 %all-to-all-start.2 = ((bf16[128,4,3584]{2,1,0:T(4,128)(2,1)}), bf16[128,4,3584]{2,1,0:T(4,128)(2,1)}, u32[]{:S(2)}, u32[]{:S(2)}) async-start(bf16[128,4,3584]{2,1,0:T(4,128)(2,1)} %reshape.415), calls=%async_computation.4 | async-start | bytes 7340032 | tf_op jit(solution)/shard_map/all_to_all | solution.py:157
  298.6 0.6 pad_clamp_fusion
  299.2 45.6 %all-to-all-done.2 = bf16[128,4,3584]{2,1,0:T(4,128)(2,1)} async-done(((bf16[128,4,3584]{2,1,0:T(4,128)(2,1)}), bf16[128,4,3584]{2,1,0:T(4,128)(2,1)}, u32[]{:S(2)}, u32[]{:S(2)}) %all-to-all-start.2) | async-done | bytes 3670048 | tf_op jit(solution)/shard_map/all_to_all | solution.py:157
  344.9 6.7 %reshape.416 = bf16[512,3584]{1,0:T(8,128)(2,1)} reshape(bf16[128,4,3584]{2,1,0:T(4,128)(2,1)} %all-to-all-done.2) | data formatting | bytes 7340032 | tf_op jit(solution)/shard_map/reshape | solution.py:165
  351.6 7.6 %gather_fusion.7 = bf16[256,3584]{1,0:T(8,128)(2,1)} fusion(bf16[512,3584]{1,0:T(8,128)(2,1)} %reshape.416, s32[1024]{0:T(1024)} %pad_clamp_fusion), kind=kCustom, calls=%fused_computation.7 | custom fusion | bytes 3671040 | tf_op jit(solution)/shard_map/gather | solution.py:165
  359.2 3.0 fusion.11
  362.2 0.7 add_convert_fusion
  362.9 1.8 reshape.417
  (78 shorter events, 1.3 us)
Async XLA Ops:
  7.2 7.8 %copy-start = (bf16[48,36864]{1,0:T(8,128)(2,1)S(1)}, bf16[48,36864]{1,0:T(8,128)(2,1)}, u32[]{:S(2)}) copy-start(bf16[48,36864]{1,0:T(8,128)(2,1)} %param.16) | copy-start | bytes 10616836
  7.2 3.0 copy-start.2
  7.2 144.9 %reduce-scatter.3.cloned.1.call-start = ((), (), s32[]{:S(2)}) async-start(), calls=%async_computation.5 | async-start | bytes 4587520 | tf_op jit(solution)/shard_map/reduce_scatter | solution.py:33
  39.9 3.4 copy-start.11
  39.9 3.4 copy-start.12
  99.6 2.8 copy-start.15
  102.3 2.7 copy-start.6
  108.9 43.2 %copy-start.13 = (s32[8,1,2]{0,2,1:T(2,128)S(1)}, s32[8,1,2]{0,2,1:T(2,128)}, u32[]{:S(2)}) copy-start(s32[8,1,2]{0,2,1:T(2,128)} %param.22) | copy-start | bytes 196
  108.9 43.4 %copy-start.3 = (s32[128]{0:T(128)S(1)}, s32[128]{0:T(128)}, u32[]{:S(2)}) copy-start(s32[128]{0:T(128)} %param.26) | copy-start | bytes 1540
  108.9 46.0 %copy-start.7 = (bf16[8,14336]{1,0:T(8,128)(2,1)S(1)}, bf16[8,14336]{1,0:T(8,128)(2,1)}, u32[]{:S(2)}) copy-start(bf16[8,14336]{1,0:T(8,128)(2,1)} %param.18) | copy-start | bytes 688132
  108.9 47.2 %copy-start.14 = (s32[1,2]{1,0:T(1,128)S(1)}, s32[1,2]{1,0:T(1,128)}, u32[]{:S(2)}) copy-start(s32[1,2]{1,0:T(1,128)} %param.23) | copy-start | bytes 28
  108.9 67.3 %reduce-scatter.5.cloned.1.call-start = ((), (), s32[]{:S(2)}) async-start(), calls=%async_computation.6 | async-start | bytes 1146880 | tf_op jit(solution)/shard_map/reduce_scatter | solution.py:33
  178.1 4.9 %collective-permute-start = (bf16[2,28672]{1,0:T(2,128)(2,1)S(1)}, bf16[2,28672]{1,0:T(2,128)(2,1)S(1)}, u32[]{:S(2)}, u32[]{:S(2)}) collective-permute-start(bf16[2,28672]{1,0:T(2,128)(2,1)S(1)} %constant_dynamic-update-slice_fusion), channel_id=1, source_target_pairs={{0,16},{16,32},{32,48},{48,64},{64,80},{80,96},{96,112},{112,0},{1... | collective-permute-start | bytes 344072 | tf_op jit(solution)/shard_map/ppermute | solution.py:27
  183.2 4.9 %collective-permute-start.1 = (bf16[2,28672]{1,0:T(2,128)(2,1)S(1)}, bf16[2,28672]{1,0:T(2,128)(2,1)S(1)}, u32[]{:S(2)}, u32[]{:S(2)}) collective-permute-start(bf16[2,28672]{1,0:T(2,128)(2,1)S(1)} %broadcast_select_fusion), channel_id=1, source_target_pairs={{0,32},{16,48},{32,64},{48,80},{64,96},{80,112},{96,0},{112,16},{1... | collective-permute-start | bytes 344072 | tf_op jit(solution)/shard_map/ppermute | solution.py:27
  188.4 5.4 %collective-permute-start.2 = (bf16[2,28672]{1,0:T(2,128)(2,1)S(1)}, bf16[2,28672]{1,0:T(2,128)(2,1)S(1)}, u32[]{:S(2)}, u32[]{:S(2)}) collective-permute-start(bf16[2,28672]{1,0:T(2,128)(2,1)S(1)} %broadcast_select_fusion.1), channel_id=1, source_target_pairs={{0,64},{16,80},{32,96},{48,112},{64,0},{80,16},{96,32},{112,48},{1... | collective-permute-start | bytes 344072 | tf_op jit(solution)/shard_map/ppermute | solution.py:27
  194.8 1.9 copy-start.8
  195.5 1.5 copy-start.9
  197.0 10.0 %copy-start.4 = (f32[32,3584]{1,0:T(8,128)}, f32[32,3584]{1,0:T(8,128)S(1)}, u32[]{:S(2)}) copy-start(f32[32,3584]{1,0:T(8,128)S(1)} %get-tuple-element.5) | copy-start | bytes 1376260
  293.5 5.1 %copy-start.10 = (f32[32,8]{0,1:T(8,128)S(1)}, f32[32,8]{0,1:T(8,128)}, u32[]{:S(2)}) copy-start(f32[32,8]{0,1:T(8,128)} %param.25) | copy-start | bytes 3076
  293.5 51.4 %all-to-all-start.2 = ((bf16[128,4,3584]{2,1,0:T(4,128)(2,1)}), bf16[128,4,3584]{2,1,0:T(4,128)(2,1)}, u32[]{:S(2)}, u32[]{:S(2)}) async-start(bf16[128,4,3584]{2,1,0:T(4,128)(2,1)} %reshape.415), calls=%async_computation.4 | async-start | bytes 7340032 | tf_op jit(solution)/shard_map/all_to_all | solution.py:157
  351.6 13.2 %copy-start.1 = (bf16[48,36864]{1,0:T(8,128)(2,1)S(1)}, bf16[48,36864]{1,0:T(8,128)(2,1)}, u32[]{:S(2)}) copy-start(bf16[48,36864]{1,0:T(8,128)(2,1)} %param.16) | copy-start | bytes 10616836
  359.2 3.0 copy-start.5
Sparse Core Ops, SparseCore 0:
  109.0 43.0 reduce-scatter.2
  154.5 21.6 reduce-scatter.4
